TPU v7x, 32 devices: a whole 2x2x4 slice. The times are simulated.
32 devices in a mesh: rows: 8 (over y, x, core), dim: 4 (over z).
Axes of the slice: x: 2, y: 2, z: 4, core: 2. Of those that a mesh axis runs over, the one named last changes fastest.
Arguments:
- entity_table: float32 [131072, 512], P(('rows', 'dim')), may hold values from -2.5 to 2.5
- relations: float32 [822, 512], replicated, may hold values from -6 to 6
- thresholds: float32 [64], replicated, may hold values from 0.2 to 2
- head_ids: int32 [2048], replicated, may hold values from 0 to 131071
- rel_ids: int32 [2048], replicated, may hold values from 0 to 821
- thr_idx: int32 [2048], replicated, may hold values from 0 to 63
Outputs:
- serving_table: float32 [131072, 512], P('rows', 'dim')
- fraction: float32 [2048], P(('rows', 'dim'))
All inputs are finite; a program needn't handle non-finite values.
Results may differ from a plain program's by a relative error of at most 0.0011.
Values sent between devices are 32-bit elements; how exact they have to be, the bound alone decides.
A program may use at most 128 MiB of HBM per device.

v0:
```python
import jax
import jax.numpy as jnp
from jax import lax
from jax.sharding import PartitionSpec as P

sharpness = 2.0


def pick_rows(table, head_ids, start):
    count = table.shape[0]
    local = head_ids - start
    owned = (local >= 0) & (local < count)
    picked = jnp.take(table, jnp.clip(local, 0, count - 1), axis=0)
    return jnp.where(owned[:, None], picked, jnp.zeros_like(picked))


def shards(entity_table, relations, thresholds, head_ids, rel_ids, thr_idx):
    local_rows = entity_table.shape[0]
    width = entity_table.shape[1]
    total_ents = local_rows * lax.axis_size("rows") * lax.axis_size("dim")
    serving = lax.all_to_all(entity_table, "dim", split_axis=1, concat_axis=0, tiled=True)
    start = (lax.axis_index("rows") * lax.axis_size("dim") + lax.axis_index("dim")) * local_rows
    partial_value = pick_rows(entity_table, head_ids, start)
    head_vecs = lax.psum(partial_value, ("rows", "dim"))
    query = (head_vecs * jnp.take(relations, rel_ids, axis=0)).astype(jnp.bfloat16)
    ent_low = entity_table.astype(jnp.bfloat16)
    level = jnp.take(thresholds, thr_idx)
    queries = query.shape[0]
    query_blocks = query.reshape(queries // 512, 512, width)
    level_blocks = level.reshape(queries // 512, 512)

    def score_block(pair):
        rows_q, rows_level = pair
        score = jnp.dot(rows_q, ent_low.T, preferred_element_type=jnp.float32)
        soft = jax.nn.sigmoid(sharpness * (score - rows_level[:, None]))
        return jnp.sum(soft, axis=1) * (1.0 / total_ents)

    partial_share = lax.map(score_block, (query_blocks, level_blocks)).reshape(queries)
    fraction = lax.psum_scatter(partial_share, ("rows", "dim"), scatter_dimension=0, tiled=True)
    return (serving, fraction)


def solution(mesh):
    placed = (P(("rows", "dim"), None), P(), P(), P(), P(), P())
    return jax.shard_map(
        shards,
        mesh=mesh,
        in_specs=placed,
        out_specs=(P("rows", "dim"), P(("rows", "dim"))),
        check_vma=False,
    )
```

profile of v0, /device:TPU:0, one launch (start us, length us, event | category | flops | bytes accessed | tf_op | source)
XLA Modules:
  0.0 399.6 jit_solution(839341070260288952)
XLA Ops:
  7.2 0.0 copy-start
  7.2 7.4 %copy_bitcast_fusion = f32[4096,4,128]{2,0,1:T(8,128)} fusion(f32[4096,512]{1,0:T(8,128)} %param.8), kind=kLoop, calls=%fused_computation.9 | loop fusion | bytes 16777216 | tf_op jit(solution)/shard_map/all_to_all | solution.py:21
  14.6 6.5 %all-to-all-start = ((f32[4096,4,128]{2,0,1:T(8,128)}), f32[4096,4,128]{2,0,1:T(8,128)}, u32[]{:S(2)}, u32[]{:S(2)}) async-start(f32[4096,4,128]{2,0,1:T(8,128)} %copy_bitcast_fusion), calls=%async_computation | async-start | bytes 16777216 | tf_op jit(solution)/shard_map/all_to_all | solution.py:21
  21.1 0.0 copy-done.3
  21.1 12.9 %gather_fusion = f32[2048,512]{1,0:T(8,128)} fusion(f32[4096,512]{1,0:T(8,128)} %param.8, s32[2048]{0:T(1024)S(1)} %fusion.5), kind=kCustom, calls=%fused_computation | custom fusion | bytes 8396800 | tf_op jit(solution)/shard_map/jit(_take)/gather | solution.py:13
  34.1 3.9 select_select_fusion
  38.0 0.0 all-reduce.3.cloned.1.call-update
  38.0 0.0 copy-start.1
  38.0 0.0 copy-start.4
  38.1 0.0 copy-start.2
  38.1 5.9 %convert_element_type.7 = bf16[4096,512]{1,0:T(8,128)(2,1)} convert(f32[4096,512]{1,0:T(8,128)} %param.8) | non-fusion elementwise | flops 2097152 | bytes 12582912 | tf_op jit(solution)/shard_map/convert_element_type | solution.py:26
  44.0 0.7 fusion.9
  44.6 0.7 fusion.7
  45.4 0.7 fusion.6
  46.1 0.7 fusion.8
  46.8 39.9 %select_select_fusion.1 = f32[2048]{0:T(1024)S(1)} fusion(s32[2048]{0:T(1024)S(1)} %copy-done.4, f32[]{:T(128)} %bitcast.6, f32[]{:T(128)} %bitcast.7, f32[]{:T(128)} %bitcast.8, f32[]{:T(128)} %bitcast.9, f32[]{:T(128)} %bitcast.10, f32[]{:T(128)} %bitcast.11, f32[]{:T(128)} %bitcast.12, f32[]{:T(128)} %bitcast.13, f32[]{:T(128)} %bitcast.14, f32[]{:T(128)} %bitcast.15, ...), kind=kLoop, calls=%fused_computation.15 | loop fusion | flops 272384 | bytes 16640 | tf_op jit(solution)/shard_map/jit(_take)/select_n | solution.py:27
  86.8 8.9 %gather_fusion.1 = f32[2048,512]{1,0:T(8,128)} fusion(f32[822,512]{1,0:T(8,128)S(1)} %copy-done, s32[2048]{0:T(1024)S(1)} %fusion.4), kind=kCustom, calls=%fused_computation.1 | custom fusion | bytes 8396800 | tf_op jit(solution)/shard_map/jit(_take)/gather | solution.py:25
  95.7 223.5 %all-reduce.3.cloned.1.call-done = f32[2048,512]{1,0:T(8,128)} async-done(((f32[2048,512]{1,0:T(8,128)}), f32[2048,512]{1,0:T(8,128)}) %all-reduce.3.cloned.1.call-update) | async-done | bytes 4194320 | tf_op jit(solution)/shard_map/psum | solution.py:24
  319.2 4.7 %multiply_convert_fusion = bf16[2048,512]{1,0:T(8,128)(2,1)} fusion(f32[2048,512]{1,0:T(8,128)} %all-reduce.3.cloned.1.call-done, f32[2048,512]{1,0:T(8,128)} %gather_fusion.1, pred[2048]{0:T(1024)(128)(4,1)S(1)} %compare_and_fusion), kind=kLoop, calls=%fused_computation.10 | loop fusion | flops 3145728 | bytes 10487808 | tf_op jit(solution)/shard_map/convert_element_type | solution.py:25
  323.9 22.9 %while.10 = (s32[]{:T(128)}, f32[4,512]{1,0:T(4,128)S(1)}, bf16[4,512,512]{2,1,0:T(8,128)(2,1)}, bf16[4096,512]{1,0:T(8,128)(2,1)}, f32[4,512]{1,0:T(4,128)S(1)}, /*index=5*/s32[]{:T(128)}, s32[]{:T(128)}) while((s32[]{:T(128)}, f32[4,512]{1,0:T(4,128)S(1)}, bf16[4,512,512]{2,1,0:T(8,128)(2,1)}, bf16[4096,512]{1,0:T(8,128)(2,1)}, ...), condition=%wide.region_3.4_spmd, body=%wide.region_1.3_spmd.sunk | while | flops 2160066560 | bytes 4735073 | solution.py:38
  323.9 5.6 %fusion.17 = f32[512]{0:T(512)S(1)} fusion(bf16[4096,512]{1,0:T(8,128)(2,1)} %get-tuple-element.154, f32[512]{0:T(512)S(1)} %bitcast.91, bf16[4,512,512]{2,1,0:T(8,128)(2,1)} %get-tuple-element.153, s32[]{:T(128)S(6)} %copy.17), kind=kOutput, calls=%fused_computation.3.clone.1 | convolution fusion | flops 2160066048 | bytes 4722692 | tf_op jit(solution)/shard_map/while/body/eval_jaxpr/dot_general | solution.py:34
  329.6 0.1 dynamic_update_slice.5
  329.6 5.6 %fusion.17 = f32[512]{0:T(512)S(1)} fusion(bf16[4096,512]{1,0:T(8,128)(2,1)} %get-tuple-element.154, f32[512]{0:T(512)S(1)} %bitcast.91, bf16[4,512,512]{2,1,0:T(8,128)(2,1)} %get-tuple-element.153, s32[]{:T(128)S(6)} %copy.17), kind=kOutput, calls=%fused_computation.3.clone.1 | convolution fusion | flops 2160066048 | bytes 4722692 | tf_op jit(solution)/shard_map/while/body/eval_jaxpr/dot_general | solution.py:34
  335.3 0.1 dynamic_update_slice.5
  335.4 5.6 %fusion.17 = f32[512]{0:T(512)S(1)} fusion(bf16[4096,512]{1,0:T(8,128)(2,1)} %get-tuple-element.154, f32[512]{0:T(512)S(1)} %bitcast.91, bf16[4,512,512]{2,1,0:T(8,128)(2,1)} %get-tuple-element.153, s32[]{:T(128)S(6)} %copy.17), kind=kOutput, calls=%fused_computation.3.clone.1 | convolution fusion | flops 2160066048 | bytes 4722692 | tf_op jit(solution)/shard_map/while/body/eval_jaxpr/dot_general | solution.py:34
  341.0 0.1 dynamic_update_slice.5
  341.1 5.6 %fusion.17 = f32[512]{0:T(512)S(1)} fusion(bf16[4096,512]{1,0:T(8,128)(2,1)} %get-tuple-element.154, f32[512]{0:T(512)S(1)} %bitcast.91, bf16[4,512,512]{2,1,0:T(8,128)(2,1)} %get-tuple-element.153, s32[]{:T(128)S(6)} %copy.17), kind=kOutput, calls=%fused_computation.3.clone.1 | convolution fusion | flops 2160066048 | bytes 4722692 | tf_op jit(solution)/shard_map/while/body/eval_jaxpr/dot_general | solution.py:34
  346.8 0.1 dynamic_update_slice.5
  346.8 39.4 %all-reduce = f32[2048]{0:T(1024)S(1)} all-reduce(f32[2048]{0:T(1024)S(1)} %bitcast.92), channel_id=2, replica_groups=mesh['rows'=8,'dim'=4] {'rows','dim'}, use_global_device_ids=true, to_apply=%region_4.5.clone | all-reduce | flops 2048 | bytes 16384
  386.3 0.6 dynamic-slice
  386.9 0.0 all-to-all-done
  386.9 5.9 %copy.22 = f32[16384,128]{1,0:T(8,128)} copy(f32[16384,128]{1,0:T(8,128)} %bitcast.4) | data formatting | bytes 16777216
  (21 shorter events, 0.1 us)
Async XLA Ops:
  7.2 79.7 %copy-start = (f32[822,512]{1,0:T(8,128)S(1)}, f32[822,512]{1,0:T(8,128)}, u32[]{:S(2)}) copy-start(f32[822,512]{1,0:T(8,128)} %param.9) | copy-start | bytes 5050372
  14.6 6.5 %copy-start.3 = (s32[2048]{0:T(1024)S(1)}, s32[2048]{0:T(1024)}, u32[]{:S(2)}) copy-start(s32[2048]{0:T(1024)} %param.11) | copy-start | bytes 24580
  14.6 372.2 %all-to-all-start = ((f32[4096,4,128]{2,0,1:T(8,128)}), f32[4096,4,128]{2,0,1:T(8,128)}, u32[]{:S(2)}, u32[]{:S(2)}) async-start(f32[4096,4,128]{2,0,1:T(8,128)} %copy_bitcast_fusion), calls=%async_computation | async-start | bytes 16777216 | tf_op jit(solution)/shard_map/all_to_all | solution.py:21
  21.1 298.1 %all-reduce.3.cloned.1.call-start = ((), (), s32[]{:S(2)}) async-start(), calls=%async_computation.1 | async-start | bytes 8388608 | tf_op jit(solution)/shard_map/psum | solution.py:24
  38.0 5.9 %copy-start.1 = (f32[64]{0:T(128)S(1)}, f32[64]{0:T(128)}, u32[]{:S(2)}) copy-start(f32[64]{0:T(128)} %param.10) | copy-start | bytes 772
  38.0 8.8 %copy-start.4 = (s32[2048]{0:T(1024)S(1)}, s32[2048]{0:T(1024)}, u32[]{:S(2)}) copy-start(s32[2048]{0:T(1024)} %param.13) | copy-start | bytes 24580
  38.1 48.7 %copy-start.2 = (s32[2048]{0:T(1024)S(1)}, s32[2048]{0:T(1024)}, u32[]{:S(2)}) copy-start(s32[2048]{0:T(1024)} %param.12) | copy-start | bytes 24580
Sparse Core Ops, SparseCore 0:
  38.1 280.9 all-reduce.2
where the time goes:
time: 401 us; the launch traced here: 400 us
  waiting for transfers between devices  223 us (56%)
  other arithmetic  54.6 us (14%)
  blocking collectives  39.4 us (10%)
  local copies, waits for them, and re-layouts  38.8 us (10%)
  matrix products  22.6 us (6%)
  between operations  14.2 us (4%)
  starting transfers between devices  6.48 us (2%)
    psum x1, waiting for transfers between devices, shards(): head_vecs = lax.psum(partial_value, ('rows', 'dim'))  223 us
    select_n x1, other arithmetic, shards(): level = jnp.take(thresholds, thr_idx)  39.9 us
    unnamed x1, blocking collectives  39.4 us
    dot_general x4, matrix products, score_block(): score = jnp.dot(rows_q, ent_low.T, preferred_element_type=jnp.float32)  22.6 us
    gather x1, local copies, waits for them, and re-layouts, pick_rows(): picked = jnp.take(table, jnp.clip(local, 0, count - 1), axis=0)  12.9 us
    gather x1, local copies, waits for them, and re-layouts, shards(): jnp.take(relations, rel_ids, axis=0)  8.85 us
  transfers between devices with their start and end apart: 2, of which 1 were waited for; matrix products, arithmetic and copies ran while one was open for 26% of the time, Pallas kernels for 0%

commit v1 on v0

--- a/solution.py
+++ b/solution.py
@@ -21,7 +21,9 @@
     serving = lax.all_to_all(entity_table, "dim", split_axis=1, concat_axis=0, tiled=True)
     start = (lax.axis_index("rows") * lax.axis_size("dim") + lax.axis_index("dim")) * local_rows
     partial_value = pick_rows(entity_table, head_ids, start)
-    head_vecs = lax.psum(partial_value, ("rows", "dim"))
+    head_vecs = partial_value
+    for p in ("dim", "rows"):
+        head_vecs = lax.psum(head_vecs, p)
     query = (head_vecs * jnp.take(relations, rel_ids, axis=0)).astype(jnp.bfloat16)
     ent_low = entity_table.astype(jnp.bfloat16)
     level = jnp.take(thresholds, thr_idx)

time: 401 us -> 505 us (1.26)
  waiting for transfers between devices: 223 us -> 327 us
    psum x1 -> x2, waiting for transfers between devices: 223 us -> 327 us  [shards(): head_vecs = lax.psum(head_vecs, p)]
  transfers between devices with their start and end apart: 2 -> 3, of which waited for: 1 -> 2; matrix products, arithmetic and copies ran while one was open for 26% -> 18% of each run, Pallas kernels for 0% -> 0%
where the time goes in v1:
time: 505 us; the launch traced here: 504 us
  waiting for transfers between devices  327 us (65%)
  other arithmetic  55.9 us (11%)
  blocking collectives  39.4 us (8%)
  local copies, waits for them, and re-layouts  38.7 us (8%)
  matrix products  22.6 us (4%)
  between operations  14.2 us (3%)
  starting transfers between devices  6.51 us (1%)
    psum x2, waiting for transfers between devices, shards(): head_vecs = lax.psum(head_vecs, p)  327 us
    select_n x1, other arithmetic, shards(): level = jnp.take(thresholds, thr_idx)  39.8 us
    unnamed x1, blocking collectives  39.4 us
    dot_general x4, matrix products, score_block(): score = jnp.dot(rows_q, ent_low.T, preferred_element_type=jnp.float32)  22.6 us
    gather x1, local copies, waits for them, and re-layouts, pick_rows(): picked = jnp.take(table, jnp.clip(local, 0, count - 1), axis=0)  12.9 us
  transfers between devices with their start and end apart: 3, of which 2 were waited for; matrix products, arithmetic and copies ran while one was open for 18% of the time, Pallas kernels for 0%

profile of v1, /device:TPU:0, one launch (start us, length us, event | category | flops | bytes accessed | tf_op | source)
XLA Modules:
  0.0 504.2 jit_solution(10360126017225137305)
XLA Ops:
  7.2 0.0 copy-start
  7.2 0.0 all-reduce.4.cloned.1.call-start
  7.2 0.8 compare_and_fusion.2
  8.1 0.7 fusion.5
  8.8 12.9 %gather_fusion = f32[2048,512]{1,0:T(8,128)} fusion(f32[4096,512]{1,0:T(8,128)} %param.8, s32[2048]{0:T(1024)S(1)} %fusion.5), kind=kCustom, calls=%fused_computation | custom fusion | bytes 8396800 | tf_op jit(solution)/shard_map/jit(_take)/gather | solution.py:13
  21.6 3.9 select_select_fusion
  25.5 0.0 all-reduce.4.cloned.1.call-update
  25.6 7.3 %copy_bitcast_fusion = f32[4096,4,128]{2,0,1:T(8,128)} fusion(f32[4096,512]{1,0:T(8,128)} %param.8), kind=kLoop, calls=%fused_computation.9 | loop fusion | bytes 16777216 | tf_op jit(solution)/shard_map/all_to_all | solution.py:21
  32.9 6.5 %all-to-all-start = ((f32[4096,4,128]{2,0,1:T(8,128)}), f32[4096,4,128]{2,0,1:T(8,128)}, u32[]{:S(2)}, u32[]{:S(2)}) async-start(f32[4096,4,128]{2,0,1:T(8,128)} %copy_bitcast_fusion), calls=%async_computation | async-start | bytes 16777216 | tf_op jit(solution)/shard_map/all_to_all | solution.py:21
  39.4 302.2 %all-reduce.4.cloned.1.call-done = f32[2048,512]{1,0:T(8,128)} async-done(((f32[2048,512]{1,0:T(8,128)}), f32[2048,512]{1,0:T(8,128)}) %all-reduce.4.cloned.1.call-update) | async-done | bytes 4194320 | tf_op jit(solution)/shard_map/psum | solution.py:26
  341.6 0.0 all-reduce.6.cloned.1.call-update
  341.7 5.9 %convert_element_type.7 = bf16[4096,512]{1,0:T(8,128)(2,1)} convert(f32[4096,512]{1,0:T(8,128)} %param.8) | non-fusion elementwise | flops 2097152 | bytes 12582912 | tf_op jit(solution)/shard_map/convert_element_type | solution.py:28
  347.6 0.7 fusion.9
  348.2 0.7 fusion.7
  348.9 0.7 fusion.6
  349.7 0.7 fusion.8
  350.4 39.8 %select_select_fusion.1 = f32[2048]{0:T(1024)S(1)} fusion(s32[2048]{0:T(1024)S(1)} %copy-done.3, f32[]{:T(128)} %bitcast.6, f32[]{:T(128)} %bitcast.7, f32[]{:T(128)} %bitcast.8, f32[]{:T(128)} %bitcast.9, f32[]{:T(128)} %bitcast.10, f32[]{:T(128)} %bitcast.11, f32[]{:T(128)} %bitcast.12, f32[]{:T(128)} %bitcast.13, f32[]{:T(128)} %bitcast.14, f32[]{:T(128)} %bitcast.15, ...), kind=kLoop, calls=%fused_computation.15 | loop fusion | flops 272384 | bytes 16640 | tf_op jit(solution)/shard_map/jit(_take)/select_n | solution.py:29
  390.2 9.0 %gather_fusion.1 = f32[2048,512]{1,0:T(8,128)} fusion(f32[822,512]{1,0:T(8,128)S(1)} %copy-done, s32[2048]{0:T(1024)S(1)} %fusion.4), kind=kCustom, calls=%fused_computation.1 | custom fusion | bytes 8396800 | tf_op jit(solution)/shard_map/jit(_take)/gather | solution.py:27
  399.2 24.7 %all-reduce.6.cloned.1.call-done = f32[2048,512]{1,0:T(8,128)} async-done(((f32[2048,512]{1,0:T(8,128)}), f32[2048,512]{1,0:T(8,128)}) %all-reduce.6.cloned.1.call-update) | async-done | bytes 4194320 | tf_op jit(solution)/shard_map/psum | solution.py:26
  423.8 4.7 multiply_convert_fusion
  428.6 22.9 %while.10 = (s32[]{:T(128)}, f32[4,512]{1,0:T(4,128)S(1)}, bf16[4,512,512]{2,1,0:T(8,128)(2,1)}, bf16[4096,512]{1,0:T(8,128)(2,1)}, f32[4,512]{1,0:T(4,128)S(1)}, /*index=5*/s32[]{:T(128)}, s32[]{:T(128)}) while((s32[]{:T(128)}, f32[4,512]{1,0:T(4,128)S(1)}, bf16[4,512,512]{2,1,0:T(8,128)(2,1)}, bf16[4096,512]{1,0:T(8,128)(2,1)}, ...), condition=%wide.region_4.5_spmd, body=%wide.region_2.4_spmd.sunk | while | flops 2160066560 | bytes 4735073 | solution.py:40
  428.6 5.6 %fusion.17 = f32[512]{0:T(512)S(1)} fusion(bf16[4096,512]{1,0:T(8,128)(2,1)} %get-tuple-element.154, f32[512]{0:T(512)S(1)} %bitcast.91, bf16[4,512,512]{2,1,0:T(8,128)(2,1)} %get-tuple-element.153, s32[]{:T(128)S(6)} %copy.18), kind=kOutput, calls=%fused_computation.3.clone.1 | convolution fusion | flops 2160066048 | bytes 4722692 | tf_op jit(solution)/shard_map/while/body/eval_jaxpr/dot_general | solution.py:36
  434.2 0.1 dynamic_update_slice.5
  434.3 5.6 %fusion.17 = f32[512]{0:T(512)S(1)} fusion(bf16[4096,512]{1,0:T(8,128)(2,1)} %get-tuple-element.154, f32[512]{0:T(512)S(1)} %bitcast.91, bf16[4,512,512]{2,1,0:T(8,128)(2,1)} %get-tuple-element.153, s32[]{:T(128)S(6)} %copy.18), kind=kOutput, calls=%fused_computation.3.clone.1 | convolution fusion | flops 2160066048 | bytes 4722692 | tf_op jit(solution)/shard_map/while/body/eval_jaxpr/dot_general | solution.py:36
  440.0 0.1 dynamic_update_slice.5
  440.0 5.6 %fusion.17 = f32[512]{0:T(512)S(1)} fusion(bf16[4096,512]{1,0:T(8,128)(2,1)} %get-tuple-element.154, f32[512]{0:T(512)S(1)} %bitcast.91, bf16[4,512,512]{2,1,0:T(8,128)(2,1)} %get-tuple-element.153, s32[]{:T(128)S(6)} %copy.18), kind=kOutput, calls=%fused_computation.3.clone.1 | convolution fusion | flops 2160066048 | bytes 4722692 | tf_op jit(solution)/shard_map/while/body/eval_jaxpr/dot_general | solution.py:36
  445.7 0.1 dynamic_update_slice.5
  445.8 5.6 %fusion.17 = f32[512]{0:T(512)S(1)} fusion(bf16[4096,512]{1,0:T(8,128)(2,1)} %get-tuple-element.154, f32[512]{0:T(512)S(1)} %bitcast.91, bf16[4,512,512]{2,1,0:T(8,128)(2,1)} %get-tuple-element.153, s32[]{:T(128)S(6)} %copy.18), kind=kOutput, calls=%fused_computation.3.clone.1 | convolution fusion | flops 2160066048 | bytes 4722692 | tf_op jit(solution)/shard_map/while/body/eval_jaxpr/dot_general | solution.py:36
  451.4 0.1 dynamic_update_slice.5
  451.5 39.4 %all-reduce = f32[2048]{0:T(1024)S(1)} all-reduce(f32[2048]{0:T(1024)S(1)} %bitcast.92), channel_id=2, replica_groups=mesh['rows'=8,'dim'=4] {'rows','dim'}, use_global_device_ids=true, to_apply=%region_5.6.clone | all-reduce | flops 2048 | bytes 16384
  490.9 0.6 dynamic-slice
  491.5 5.9 %copy.23 = f32[16384,128]{1,0:T(8,128)} copy(f32[16384,128]{1,0:T(8,128)} %bitcast.4) | data formatting | bytes 16777216
  (22 shorter events, 0.1 us)
Async XLA Ops:
  7.2 383.0 %copy-start = (f32[822,512]{1,0:T(8,128)S(1)}, f32[822,512]{1,0:T(8,128)}, u32[]{:S(2)}) copy-start(f32[822,512]{1,0:T(8,128)} %param.9) | copy-start | bytes 5050372
  7.2 334.4 %all-reduce.4.cloned.1.call-start = ((), (), s32[]{:S(2)}) async-start(), calls=%async_computation.1 | async-start | bytes 8388608 | tf_op jit(solution)/shard_map/psum | solution.py:26
  32.9 458.6 %all-to-all-start = ((f32[4096,4,128]{2,0,1:T(8,128)}), f32[4096,4,128]{2,0,1:T(8,128)}, u32[]{:S(2)}, u32[]{:S(2)}) async-start(f32[4096,4,128]{2,0,1:T(8,128)} %copy_bitcast_fusion), calls=%async_computation | async-start | bytes 16777216 | tf_op jit(solution)/shard_map/all_to_all | solution.py:21
  39.4 384.5 %all-reduce.6.cloned.1.call-start = ((), (), s32[]{:S(2)}) async-start(), calls=%async_computation.2 | async-start | bytes 8388608 | tf_op jit(solution)/shard_map/psum | solution.py:26
  341.6 5.9 %copy-start.1 = (f32[64]{0:T(128)S(1)}, f32[64]{0:T(128)}, u32[]{:S(2)}) copy-start(f32[64]{0:T(128)} %param.10) | copy-start | bytes 772
  341.6 8.7 %copy-start.3 = (s32[2048]{0:T(1024)S(1)}, s32[2048]{0:T(1024)}, u32[]{:S(2)}) copy-start(s32[2048]{0:T(1024)} %param.13) | copy-start | bytes 24580
  341.7 48.5 %copy-start.2 = (s32[2048]{0:T(1024)S(1)}, s32[2048]{0:T(1024)}, u32[]{:S(2)}) copy-start(s32[2048]{0:T(1024)} %param.12) | copy-start | bytes 24580
Sparse Core Ops, SparseCore 0:
  25.7 315.8 all-reduce.3
  344.9 78.9 all-reduce.5
